TPU v7x, 32 devices: a whole 2x2x4 slice. The times are simulated.
32 devices in a mesh: light: 4 (over y, x), screen: 8 (over z, core).
Axes of the slice: x: 2, y: 2, z: 4, core: 2. Of those that a mesh axis runs over, the one named last changes fastest.
Arguments:
- density: float32 [128, 256, 512], P('screen', None, 'light'), may hold values from 0 to 1.09375, as said below
- albedo: float32 [128, 256, 512], P('screen', None, 'light'), may hold values from 0.2 to 1
- light_in: float32 [128, 256], replicated, may hold values from 0.5 to 1.5
- occupancy: int32 [8, 16, 32], P('screen', None, 'light'), may hold values 0 or 1
- phase: int32 [256, 512], replicated, may hold values from 0 to 15
- fractions: float32 [3, 16], replicated, may hold values from 0 to 1
Outputs:
- image: float32 [256, 512], P('screen', 'light')
- transmittance: float32 [256, 512], P('screen', 'light')
- lit_bricks: float32 [128, 256, 512], P('light', 'screen')
Inputs may be any that keep to these rules, and one draw needn't show every extreme that they name: `density`: nonnegative extinction of each cell. `occupancy`: 1 where the brick of 16 cells on a side is occupied.
All inputs are finite; a program needn't handle non-finite values. No bound on the sum of `occupancy` on one device may be relied on, other than what follows from the above.
Results may differ from a plain program's by a relative error of at most 0.0003.
Values sent between devices are 32-bit elements; how exact they have to be, the bound alone decides.
No kernel may reach another device: no remote copies, remote signals or barrier semaphores. Data moves between devices by JAX's collectives and lax.ppermute only.
A program may use at most 192 MiB of HBM per device.

v0:
```python
import jax
import jax.numpy as jnp
from jax import lax
from jax.sharding import PartitionSpec as P

BRICK = 16


def passed_along(value, axis, by):
    peers = lax.axis_size(axis)
    pairs = [(i, i + by) for i in range(peers) if 0 <= i + by < peers]
    return lax.ppermute(value, axis, pairs)


def carried_in(part, axis, combine, identity):
    place = lax.axis_index(axis)
    gathered = lax.all_gather(part, axis)
    state = jnp.zeros_like(part) + jnp.asarray(identity, part.dtype)

    def one(step, state):
        return combine(state, lax.dynamic_index_in_dim(gathered, step, 0, False))

    return lax.fori_loop(0, place, one, state)


def prefix_last(values):
    length = values.shape[-1]
    block = 128
    count = length // block
    shaped = values.reshape(values.shape[:-1] + (count, block))
    rowsidx = lax.broadcasted_iota(jnp.int32, (block, block), 0)
    colsidx = lax.broadcasted_iota(jnp.int32, (block, block), 1)
    upper = (rowsidx < colsidx).astype(jnp.float32)
    within = jnp.matmul(shaped, upper, precision=lax.Precision.HIGHEST)
    totals = jnp.sum(shaped, axis=-1)
    carried = jnp.cumsum(totals, axis=-1) - totals
    return (within + carried[..., None]).reshape(values.shape)


def prefix_first(values):
    length = values.shape[0]
    count = length // length
    shaped = values.reshape(count, length, -1)
    rowsidx = lax.broadcasted_iota(jnp.int32, (length, length), 0)
    colsidx = lax.broadcasted_iota(jnp.int32, (length, length), 1)
    lower = (colsidx < rowsidx).astype(jnp.float32)
    within = jnp.einsum("ij,bjr->bir", lower, shaped, precision=lax.Precision.HIGHEST)
    totals = jnp.sum(shaped, axis=1)
    carried = jnp.cumsum(totals, axis=0) - totals
    return (within + carried[:, None]).reshape(values.shape)


def corner_fractions(rays, fractions):
    levels = lax.broadcasted_iota(jnp.int32, (fractions.shape[1], 1, 1), 0)
    onehot = (rays[None] == levels).astype(jnp.float32)
    return jnp.einsum("kp,prc->krc", fractions, onehot, precision=lax.Precision.HIGHEST)


def resample(field, tail, weights, deep, cols):
    first = field[:, 0:cols]
    second = field[:, 1 : cols + 1]
    edge_first = tail[:, 0:cols]
    edge_second = tail[:, 1 : cols + 1]
    first_next = jnp.concatenate([first[:, :, 1:], edge_first], axis=2)
    second_next = jnp.concatenate([second[:, :, 1:], edge_second], axis=2)
    depth_w = weights[0]
    column_w = weights[1]
    light_w = weights[2]
    near = first + column_w * (second - first)
    further = first_next + column_w * (second_next - first_next)
    mixed = near + light_w * (further - near)
    lower = mixed[0:deep]
    higher = mixed[1 : deep + 1]
    return lower + depth_w * (higher - lower)


def composite(extinct, shaded):
    screened = prefix_first(extinct)
    part = jnp.sum(jnp.exp(-screened) * (1.0 - jnp.exp(-extinct)) * shaded, axis=0)
    return (part, jnp.sum(extinct, axis=0))


def finish(parts, totals):
    before = jnp.cumsum(totals, axis=0) - totals
    picture = jnp.sum(jnp.exp(-before) * parts, axis=0)
    return (picture, jnp.exp(-jnp.sum(totals, axis=0)))


def march_slabs(masked, lit, phase, fractions):
    slab_b, width_a, slab_l = masked.shape
    light_idx = lax.axis_index("light")
    rims = passed_along((masked[:2], lit[:2]), "screen", -1)
    dens_ext = jnp.pad(jnp.concatenate([masked, rims[0]], axis=0), ((0, 0), (0, 2), (0, 0)))
    lit_ext = jnp.pad(jnp.concatenate([lit, rims[1]], axis=0), ((0, 0), (0, 2), (0, 0)))
    tails = passed_along((dens_ext[:, :, :1], lit_ext[:, :, :1]), "light", -1)
    rays = lax.dynamic_slice_in_dim(phase, light_idx * slab_l, slab_l, 1)
    weights = corner_fractions(rays, fractions)
    extinct = resample(dens_ext, tails[0], weights, slab_b, width_a)
    shaded = resample(lit_ext, tails[1], weights, slab_b, width_a)
    part, total = composite(extinct, shaded)
    parts, totals = (
        lax.all_to_all(part[None], "screen", split_axis=1, concat_axis=0, tiled=True),
        lax.all_to_all(total[None], "screen", split_axis=1, concat_axis=0, tiled=True),
    )
    return finish(parts, totals)


def local(density, albedo, light_in, occupancy, phase, fractions):
    slab_b, width_a, slab_l = density.shape
    bricks_b, bricks_a, bricks_l = occupancy.shape
    masked = (
        density.reshape(bricks_b, BRICK, bricks_a, BRICK, bricks_l, BRICK)
        * occupancy.astype(jnp.float32)[:, None, :, None, :, None]
    ).reshape(density.shape)
    screen_idx = lax.axis_index("screen")
    local_depth = prefix_last(masked)
    totals = jnp.sum(masked, axis=2)
    before = carried_in(totals, "light", jnp.add, jnp.zeros_like(totals))
    incoming = lax.dynamic_slice_in_dim(light_in, screen_idx * slab_b, slab_b, 0)
    lit = albedo * incoming[:, :, None] * jnp.exp(-(local_depth + before[:, :, None]))
    lit_cam = lax.all_to_all(lit, "screen", split_axis=1, concat_axis=0, tiled=True)
    lit_cam = lax.all_to_all(lit_cam, "light", split_axis=0, concat_axis=2, tiled=True)
    picture, passing = march_slabs(masked, lit, phase, fractions)
    return (picture, passing, lit_cam)


def solution(mesh):
    return jax.shard_map(
        local,
        mesh=mesh,
        in_specs=(
            P("screen", None, "light"),
            P("screen", None, "light"),
            P(),
            P("screen", None, "light"),
            P(),
            P(),
        ),
        out_specs=(P("screen", "light"), P("screen", "light"), P("light", "screen", None)),
        check_vma=False,
    )
```

profile of v0, /device:TPU:0, one launch (start us, length us, event | category | flops | bytes accessed | tf_op | source)
XLA Modules:
  0.0 195.5 jit_solution(17380704200879934052)
XLA Ops:
  1.9 2.2 %fusion.35 = (f32[16,256]{1,0:T(8,128)S(1)}, f32[16,256,128]{2,1,0:T(8,128)S(1)}) fusion(f32[16,256,128]{2,1,0:T(8,128)} %param.8, f32[256,128]{1,0:T(8,128)S(1)} %mul.121), kind=kLoop, calls=%fused_computation.62 | loop fusion | flops 1044480 | bytes 4341760 | tf_op jit(solution)/shard_map/reduce_sum | solution.py:35
  4.2 9.7 %all-gather = f32[64,256]{1,0:T(8,128)S(1)} all-gather(f32[16,256]{1,0:T(8,128)S(1)} %get-tuple-element.35), channel_id=2, replica_groups=mesh['light'=4,'screen'=8] {'light'}, dimensions={0}, use_global_device_ids=true | all-gather | bytes 81920 | tf_op jit(solution)/shard_map/all_gather | solution.py:17
  14.6 3.8 %exponential_multiply_fusion = f32[16,256,128]{2,1,0:T(8,128)S(1)} fusion(f32[16,256,128]{2,1,0:T(8,128)} %param.9, f32[16,256,128]{2,1,0:T(8,128)S(1)} %get-tuple-element.36, f32[16,256]{1,0:T(8,128)S(1)} %get-tuple-element.26, f32[16,256]{1,0:T(8,128)S(1)} %sub.66, f32[16,256]{1,0:T(8,128)S(1)} %constant_dynamic-slice_fusion), kind=kOutput, calls=%fused_computation.42 | convolution fusion | flops 807944192 | bytes 6340608 | tf_op jit(solution)/shard_map/dot_general | solution.py:34
  21.1 10.6 %reshape.82 = f32[1,16,16,16,8,16]{5,4,3,2,1,0:T(8,128)} reshape(f32[16,256,128]{2,1,0:T(8,128)} %param.8) | data formatting | bytes 4194304 | tf_op jit(solution)/shard_map/reshape | solution.py:112
  31.7 1.9 slice_multiply_fusion
  37.9 1.7 pad_maximum_fusion.1
  39.6 2.1 %pad_slice_fusion.2 = f32[18,256,127]{2,1,0:T(8,128)} fusion(f32[18,256,128]{2,1,0:T(8,128)S(1)} %pad_maximum_fusion.1), kind=kLoop, calls=%fused_computation.25 | loop fusion | bytes 4700160 | tf_op jit(solution)/shard_map/slice | solution.py:65
  41.7 1.6 pad_slice_fusion.3
  44.4 2.2 %pad_slice_fusion.4 = f32[18,256,127]{2,1,0:T(8,128)} fusion(f32[18,256,128]{2,1,0:T(8,128)S(1)} %pad_maximum_fusion), kind=kLoop, calls=%fused_computation.27 | loop fusion | bytes 4700160 | tf_op jit(solution)/shard_map/slice | solution.py:65
  46.6 1.6 pad_slice_fusion.5
  48.2 2.7 %copy.33 = f32[18,258,1]{1,2,0:T(1,128)S(1)} copy(f32[18,258,1]{2,1,0:T(8,128)} %pad_slice_fusion.3) | data formatting | bytes 37152 | tf_op jit(solution)/shard_map/slice | solution.py:95
  52.2 2.7 %copy.30 = f32[18,258,1]{1,2,0:T(1,128)S(1)} copy(f32[18,258,1]{2,1,0:T(8,128)} %pad_slice_fusion.5) | data formatting | bytes 37152 | tf_op jit(solution)/shard_map/slice | solution.py:95
  56.5 3.7 %fusion.3 = f32[18,256,127]{2,1,0:T(8,128)} fusion(f32[2,256,128]{2,1,0:T(8,128)S(1)} %collective-permute-done.2, f32[16,256,128]{2,1,0:T(8,128)} %copy-done.3), kind=kLoop, calls=%fused_computation.9 | loop fusion | flops 585216 | bytes 4700160 | tf_op jit(solution)/shard_map/concatenate | solution.py:94
  60.2 2.1 %fusion.4 = f32[18,256,127]{2,1,0:T(8,128)} fusion(f32[2,256,128]{2,1,0:T(8,128)S(1)} %collective-permute-done, f32[16,256,128]{2,1,0:T(8,128)S(1)} %copy-done.7), kind=kLoop, calls=%fused_computation.10 | loop fusion | flops 585216 | bytes 4700160 | tf_op jit(solution)/shard_map/concatenate | solution.py:93
  62.4 2.1 %copy.35 = f32[18,256,1]{2,1,0:T(8,128)} copy(f32[18,256,1]{1,2,0:T(1,128)S(1)} %get-tuple-element.44) | data formatting | bytes 36864 | tf_op jit(solution)/shard_map/slice | solution.py:63
  64.6 2.2 %copy.34 = f32[18,256,1]{2,1,0:T(8,128)} copy(f32[18,256,1]{1,2,0:T(1,128)S(1)} %get-tuple-element.45) | data formatting | bytes 36864 | tf_op jit(solution)/shard_map/slice | solution.py:62
  66.8 2.1 %copy.32 = f32[18,256,1]{2,1,0:T(8,128)} copy(f32[18,256,1]{1,2,0:T(1,128)S(1)} %get-tuple-element.46) | data formatting | bytes 36864 | tf_op jit(solution)/shard_map/slice | solution.py:63
  69.0 2.1 %copy.31 = f32[18,256,1]{2,1,0:T(8,128)} copy(f32[18,256,1]{1,2,0:T(1,128)S(1)} %get-tuple-element.47) | data formatting | bytes 36864 | tf_op jit(solution)/shard_map/slice | solution.py:62
  71.1 12.0 %fusion.14 = (f32[18,256,128]{2,1,0:T(8,128)}, f32[18,256,128]{2,1,0:T(8,128)S(1)}) fusion(f32[18,256,1]{2,1,0:T(8,128)} %copy.34, f32[18,256,127]{2,1,0:T(8,128)} %fusion.3, f32[18,256,1]{2,1,0:T(8,128)} %copy.35, f32[18,256,127]{2,1,0:T(8,128)} %pad_slice_fusion.2, f32[18,256,128]{2,1,0:T(8,128)S(1)} %pad_maximum_fusion.1, f32[256,128]{1,0:T(8,128)S(1)} %bitcast.74, ...), kind=kLoop, calls=%fused_computation.24 | loop fusion | flops 12976128 | bytes 19136512 | tf_op jit(solution)/shard_map/add | solution.py:71
  83.2 2.3 %fusion.36 = (f32[256,128]{1,0:T(8,128)}, f32[16,256,128]{2,1,0:T(8,128)}) fusion(f32[18,256,128]{2,1,0:T(8,128)S(1)} %get-tuple-element.43, f32[256,128]{1,0:T(8,128)S(1)} %bitcast.72), kind=kLoop, calls=%fused_computation.63 | loop fusion | flops 2064384 | bytes 6553600 | tf_op jit(solution)/shard_map/reduce_sum | solution.py:80
  85.5 6.7 %all-to-all-start = ((f32[1,256,128]{2,0,1:T(1,128)}), f32[1,256,128]{2,0,1:T(1,128)S(1)}, u32[]{:S(2)}, u32[]{:S(2)}) async-start(f32[1,256,128]{2,0,1:T(1,128)} %bitcast.7), calls=%async_computation | async-start | bytes 262144 | tf_op jit(solution)/shard_map/all_to_all | solution.py:103
  92.2 2.5 %copy.36 = f32[16,256,128]{2,0,1:T(8,128)} copy(f32[16,256,128]{2,1,0:T(8,128)S(1)} %copy-done.4) | data formatting | bytes 4194304 | tf_op jit(solution)/shard_map/mul | solution.py:120
  94.7 4.2 %all-to-all-done = f32[1,256,128]{2,0,1:T(1,128)S(1)} async-done(((f32[1,256,128]{2,0,1:T(1,128)}), f32[1,256,128]{2,0,1:T(1,128)S(1)}, u32[]{:S(2)}, u32[]{:S(2)}) %all-to-all-start) | async-done | bytes 131104 | tf_op jit(solution)/shard_map/all_to_all | solution.py:103
  98.9 4.4 %all-to-all-start.2 = ((f32[16,256,128]{2,0,1:T(8,128)}), f32[16,256,128]{2,0,1:T(8,128)}, u32[]{:S(2)}, u32[]{:S(2)}) async-start(f32[16,256,128]{2,0,1:T(8,128)} %copy.36), calls=%async_computation.2 | async-start | bytes 4194304 | tf_op jit(solution)/shard_map/all_to_all | solution.py:121
  104.2 2.5 %fusion.24 = f32[2,8,256,128]{3,1,2,0:T(8,128)S(1)} fusion(f32[2,8,256,128]{3,2,1,0:T(8,128)S(1)} %bitcast.67, f32[32768]{0:T(1024)S(1)} %subtract_bitcast_fusion), kind=kOutput, calls=%fused_computation.45 | convolution fusion | flops 101712128 | bytes 4325376 | tf_op jit(solution)/shard_map/ij,bjr->bir/dot_general | solution.py:47
  109.7 42.7 %all-to-all-done.2 = f32[16,256,128]{2,0,1:T(8,128)} async-done(((f32[16,256,128]{2,0,1:T(8,128)}), f32[16,256,128]{2,0,1:T(8,128)}, u32[]{:S(2)}, u32[]{:S(2)}) %all-to-all-start.2) | async-done | bytes 2097184 | tf_op jit(solution)/shard_map/all_to_all | solution.py:121
  152.3 3.4 %all-to-all-start.1 = ((f32[1,256,128]{2,0,1:T(1,128)}), f32[1,256,128]{2,0,1:T(1,128)S(1)}, u32[]{:S(2)}, u32[]{:S(2)}) async-start(f32[1,256,128]{2,0,1:T(1,128)} %bitcast.14), calls=%async_computation.1 | async-start | bytes 262144 | tf_op jit(solution)/shard_map/all_to_all | solution.py:102
  155.7 3.5 %copy.38 = f32[8,16,32,128]{3,2,1,0:T(8,128)} copy(f32[8,16,32,128]{3,1,2,0:T(8,128)} %bitcast.18) | data formatting | bytes 4194304 | tf_op jit(solution)/shard_map/all_to_all | solution.py:121
  159.3 3.1 %all-to-all-done.1 = f32[1,256,128]{2,0,1:T(1,128)S(1)} async-done(((f32[1,256,128]{2,0,1:T(1,128)}), f32[1,256,128]{2,0,1:T(1,128)S(1)}, u32[]{:S(2)}, u32[]{:S(2)}) %all-to-all-start.1) | async-done | bytes 131104 | tf_op jit(solution)/shard_map/all_to_all | solution.py:102
  162.4 6.9 %all-to-all-start.3 = ((f32[128,32,128]{2,1,0:T(8,128)}), f32[128,32,128]{2,1,0:T(8,128)S(1)}, u32[]{:S(2)}, u32[]{:S(2)}) async-start(f32[128,32,128]{2,1,0:T(8,128)} %bitcast.19), calls=%async_computation.3 | async-start | bytes 4194304 | tf_op jit(solution)/shard_map/all_to_all | solution.py:122
  170.6 23.3 %all-to-all-done.3 = f32[128,32,128]{2,1,0:T(8,128)S(1)} async-done(((f32[128,32,128]{2,1,0:T(8,128)}), f32[128,32,128]{2,1,0:T(8,128)S(1)}, u32[]{:S(2)}, u32[]{:S(2)}) %all-to-all-start.3) | async-done | bytes 2097184 | tf_op jit(solution)/shard_map/all_to_all | solution.py:122
  193.9 1.6 copy.51
  (56 shorter events, 18.2 us)
Async XLA Ops:
  0.6 35.5 %copy-start = (s32[256,512]{1,0:T(8,128)S(1)}, s32[256,512]{1,0:T(8,128)}, u32[]{:S(2)}) copy-start(s32[256,512]{1,0:T(8,128)} %param.12) | copy-start | bytes 1572868
  4.1 14.3 %copy-start.5 = (f32[16,256,128]{2,1,0:T(8,128)}, f32[16,256,128]{2,1,0:T(8,128)S(1)}, u32[]{:S(2)}) copy-start(f32[16,256,128]{2,1,0:T(8,128)S(1)} %get-tuple-element.36) | copy-start | bytes 6291460
  18.5 1.3 copy-start.3
  19.8 18.1 %collective-permute-start.2 = (f32[2,256,128]{2,1,0:T(8,128)S(1)}, f32[2,256,128]{2,1,0:T(8,128)S(1)}, u32[]{:S(2)}, u32[]{:S(2)}) collective-permute-start(f32[2,256,128]{2,1,0:T(8,128)S(1)} %slice.105), channel_id=1, source_target_pairs={{1,0},{2,1},{3,2},{4,3},{5,4},{6,5},{7,6},{9,8},{10,9},{11,10},{12... | collective-permute-start | bytes 786440 | tf_op jit(solution)/shard_map/ppermute | solution.py:12
  33.6 2.6 %copy-start.12 = (f32[3,16]{1,0:T(4,128)S(1)}, f32[3,16]{1,0:T(4,128)}, u32[]{:S(2)}) copy-start(f32[3,16]{1,0:T(4,128)} %param.13) | copy-start | bytes 580
  34.8 8.5 %collective-permute-start = (f32[2,256,128]{2,1,0:T(8,128)}, f32[2,256,128]{2,1,0:T(8,128)S(1)}, u32[]{:S(2)}, u32[]{:S(2)}) collective-permute-start(f32[2,256,128]{2,1,0:T(8,128)} %slice.74), channel_id=1, source_target_pairs={{1,0},{2,1},{3,2},{4,3},{5,4},{6,5},{7,6},{9,8},{10,9},{11,10},{12... | collective-permute-start | bytes 786440 | tf_op jit(solution)/shard_map/ppermute | solution.py:12
  41.7 2.5 %copy-start.6 = (f32[16,256,128]{2,1,0:T(8,128)S(1)}, f32[16,256,128]{2,1,0:T(8,128)}, u32[]{:S(2)}) copy-start(f32[16,256,128]{2,1,0:T(8,128)} %copy-done.5) | copy-start | bytes 6291460
  44.4 2.2 %copy-start.2 = (f32[18,256,128]{2,1,0:T(8,128)}, f32[18,256,128]{2,1,0:T(8,128)S(1)}, u32[]{:S(2)}) copy-start(f32[18,256,128]{2,1,0:T(8,128)S(1)} %pad_maximum_fusion) | copy-start | bytes 7077892
  50.9 11.4 %collective-permute-start.3 = (f32[18,258,1]{1,2,0:T(1,128)S(1)}, f32[18,258,1]{1,2,0:T(1,128)S(1)}, u32[]{:S(2)}, u32[]{:S(2)}) collective-permute-start(f32[18,258,1]{1,2,0:T(1,128)S(1)} %copy.33), channel_id=1, source_target_pairs={{8,0},{16,8},{24,16},{9,1},{17,9},{25,17},{10,2},{18,10},{26,18},{... | collective-permute-start | bytes 55736 | tf_op jit(solution)/shard_map/ppermute | solution.py:12
  54.9 5.3 %copy-start.7 = (f32[16,256,128]{2,1,0:T(8,128)S(1)}, f32[16,256,128]{2,1,0:T(8,128)}, u32[]{:S(2)}) copy-start(f32[16,256,128]{2,1,0:T(8,128)} %copy-done.5) | copy-start | bytes 6291460
  54.9 11.8 %collective-permute-start.1 = (f32[18,258,1]{1,2,0:T(1,128)S(1)}, f32[18,258,1]{1,2,0:T(1,128)S(1)}, u32[]{:S(2)}, u32[]{:S(2)}) collective-permute-start(f32[18,258,1]{1,2,0:T(1,128)S(1)} %copy.30), channel_id=1, source_target_pairs={{8,0},{16,8},{24,16},{9,1},{17,9},{25,17},{10,2},{18,10},{26,18},{... | collective-permute-start | bytes 55736 | tf_op jit(solution)/shard_map/ppermute | solution.py:12
  66.8 4.3 %copy-start.10 = (f32[1,256,128]{2,0,1:T(1,128)S(1)}, f32[1,256,128]{2,0,1:T(1,128)}, u32[]{:S(2)}) copy-start(f32[1,256,128]{2,0,1:T(1,128)} %get-tuple-element.40) | copy-start | bytes 393220
  66.8 4.3 %copy-start.11 = (f32[1,256,128]{2,0,1:T(1,128)S(1)}, f32[1,256,128]{2,0,1:T(1,128)}, u32[]{:S(2)}) copy-start(f32[1,256,128]{2,0,1:T(1,128)} %get-tuple-element.41) | copy-start | bytes 393220
  83.2 9.0 %copy-start.4 = (f32[16,256,128]{2,1,0:T(8,128)S(1)}, f32[16,256,128]{2,1,0:T(8,128)}, u32[]{:S(2)}) copy-start(f32[16,256,128]{2,1,0:T(8,128)} %copy-done.3) | copy-start | bytes 6291460
  85.5 13.4 %all-to-all-start = ((f32[1,256,128]{2,0,1:T(1,128)}), f32[1,256,128]{2,0,1:T(1,128)S(1)}, u32[]{:S(2)}, u32[]{:S(2)}) async-start(f32[1,256,128]{2,0,1:T(1,128)} %bitcast.7), calls=%async_computation | async-start | bytes 262144 | tf_op jit(solution)/shard_map/all_to_all | solution.py:103
  94.7 9.5 %copy-start.8 = (f32[16,256,128]{2,1,0:T(8,128)S(1)}, f32[16,256,128]{2,1,0:T(8,128)}, u32[]{:S(2)}) copy-start(f32[16,256,128]{2,1,0:T(8,128)} %get-tuple-element.38) | copy-start | bytes 6291460
  98.9 53.4 %all-to-all-start.2 = ((f32[16,256,128]{2,0,1:T(8,128)}), f32[16,256,128]{2,0,1:T(8,128)}, u32[]{:S(2)}, u32[]{:S(2)}) async-start(f32[16,256,128]{2,0,1:T(8,128)} %copy.36), calls=%async_computation.2 | async-start | bytes 4194304 | tf_op jit(solution)/shard_map/all_to_all | solution.py:121
  106.7 1.7 copy-start.9
  152.3 10.1 %all-to-all-start.1 = ((f32[1,256,128]{2,0,1:T(1,128)}), f32[1,256,128]{2,0,1:T(1,128)S(1)}, u32[]{:S(2)}, u32[]{:S(2)}) async-start(f32[1,256,128]{2,0,1:T(1,128)} %bitcast.14), calls=%async_computation.1 | async-start | bytes 262144 | tf_op jit(solution)/shard_map/all_to_all | solution.py:102
  162.4 31.5 %all-to-all-start.3 = ((f32[128,32,128]{2,1,0:T(8,128)}), f32[128,32,128]{2,1,0:T(8,128)S(1)}, u32[]{:S(2)}, u32[]{:S(2)}) async-start(f32[128,32,128]{2,1,0:T(8,128)} %bitcast.19), calls=%async_computation.3 | async-start | bytes 4194304 | tf_op jit(solution)/shard_map/all_to_all | solution.py:122
  169.4 26.2 %copy-start.1 = (s32[256,512]{1,0:T(8,128)S(1)}, s32[256,512]{1,0:T(8,128)}, u32[]{:S(2)}) copy-start(s32[256,512]{1,0:T(8,128)} %param.12) | copy-start | bytes 1572868
where the time goes:
time: 197 us; the launch traced here: 196 us
  waiting for transfers between devices  73.3 us (37%)
  local copies, waits for them, and re-layouts  47.3 us (24%)
  other arithmetic  30.4 us (15%)
  starting transfers between devices  26.8 us (14%)
  blocking collectives  9.72 us (5%)
  matrix products  7 us (4%)
    all_to_all x1, waiting for transfers between devices, local(): lax.all_to_all(lit, 'screen', split_axis=1, concat_axis=0, tiled=True)  42.7 us
    all_to_all x1, waiting for transfers between devices, local(): lax.all_to_all(lit_cam, 'light', split_axis=0, concat_axis=2, tiled=True)  23.3 us
    add x1, other arithmetic, resample(): mixed = near + light_w * (further - near)  12 us
    reshape x1, local copies, waits for them, and re-layouts, local(): density.reshape(bricks_b, BRICK, bricks_a, BRICK, bricks_l, BRICK)  10.6 us
    all_gather x1, blocking collectives, carried_in(): gathered = lax.all_gather(part, axis)  9.72 us
    slice x4, local copies, waits for them, and re-layouts, march_slabs(): tails = passed_along((dens_ext[:, :, :1], lit_ext[:, :, :1]), 'light', -1)  8.64 us
    all_to_all x1, starting transfers between devices, local(): lax.all_to_all(lit_cam, 'light', split_axis=0, concat_axis=2, tiled=True)  6.94 us
    all_to_all x1, starting transfers between devices, march_slabs(): lax.all_to_all(total[None], 'screen', split_axis=1, concat_axis=0, tiled=...  6.67 us
  transfers between devices with their start and end apart: 8, of which 4 were waited for; matrix products, arithmetic and copies ran while one was open for 24% of the time, Pallas kernels for 0%

commit v1 on v0

--- a/solution.py
+++ b/solution.py
@@ -119,7 +119,12 @@
     incoming = lax.dynamic_slice_in_dim(light_in, screen_idx * slab_b, slab_b, 0)
     lit = albedo * incoming[:, :, None] * jnp.exp(-(local_depth + before[:, :, None]))
     lit_cam = lax.all_to_all(lit, "screen", split_axis=1, concat_axis=0, tiled=True)
-    lit_cam = lax.all_to_all(lit_cam, "light", split_axis=0, concat_axis=2, tiled=True)
+    lit_cam = jnp.concatenate(
+        lax.all_to_all(
+            jnp.stack(jnp.split(lit_cam, lax.axis_size("light"), axis=0)), "light", 0, 0
+        ),
+        axis=2,
+    )
     picture, passing = march_slabs(masked, lit, phase, fractions)
     return (picture, passing, lit_cam)
 

time: 197 us -> 177 us (0.90)
  waiting for transfers between devices: 73.3 us -> 29.2 us
  starting transfers between devices: 26.8 us -> 51.8 us
  local copies, waits for them, and re-layouts: 47.3 us -> 43.7 us
  other arithmetic: 30.4 us -> 33.4 us
    all_to_all x1, waiting for transfers between devices: 42.7 us -> 0.01 us  [local(): lax.all_to_all(lit, 'screen', split_axis=1, concat_axis=0, tiled=True)]
    all_to_all x1, starting transfers between devices: 6.67 us -> 31 us  [march_slabs(): lax.all_to_all(total[None], 'screen', split_axis=1, concat_axis=0, tiled=...]
    all_to_all x1, waiting for transfers between devices: 4.2 us -> 0.18 us  [march_slabs(): lax.all_to_all(total[None], 'screen', split_axis=1, concat_axis=0, tiled=...]
    reduce_sum x1, other arithmetic: 1.29 us -> 4.3 us  [composite(): jnp.sum(jnp.exp(-screened) * (1.0 - jnp.exp(-extinct)) * shaded, axis=0)]
    all_to_all x1, starting transfers between devices: 6.94 us -> 4.63 us  [local(): lax.all_to_all(jnp.stack(jnp.split(lit_cam, lax.axis_size('light'), axis=...]
    reshape x1, local copies, waits for them, and re-layouts: 10.6 us -> 8.47 us  [local(): density.reshape(bricks_b, BRICK, bricks_a, BRICK, bricks_l, BRICK)]
  transfers between devices with their start and end apart: 8 -> 8, of which waited for: 4 -> 3; matrix products, arithmetic and copies ran while one was open for 24% -> 41% of each run, Pallas kernels for 0% -> 0%
where the time goes in v1:
time: 177 us; the launch traced here: 176 us
  starting transfers between devices  51.8 us (29%)
  local copies, waits for them, and re-layouts  43.7 us (25%)
  other arithmetic  33.4 us (19%)
  waiting for transfers between devices  29.2 us (16%)
  blocking collectives  9.72 us (5%)
  matrix products  7 us (4%)
    all_to_all x1, starting transfers between devices, march_slabs(): lax.all_to_all(total[None], 'screen', split_axis=1, concat_axis=0, tiled=...  31 us
    all_to_all x1, waiting for transfers between devices, local(): lax.all_to_all(jnp.stack(jnp.split(lit_cam, lax.axis_size('light'), axis=...  24.1 us
    add x1, other arithmetic, resample(): mixed = near + light_w * (further - near)  11.8 us
    all_gather x1, blocking collectives, carried_in(): gathered = lax.all_gather(part, axis)  9.72 us
    slice x4, local copies, waits for them, and re-layouts, march_slabs(): tails = passed_along((dens_ext[:, :, :1], lit_ext[:, :, :1]), 'light', -1)  8.67 us
    reshape x1, local copies, waits for them, and re-layouts, local(): density.reshape(bricks_b, BRICK, bricks_a, BRICK, bricks_l, BRICK)  8.47 us
    all_to_all x1, starting transfers between devices, local(): lax.all_to_all(lit, 'screen', split_axis=1, concat_axis=0, tiled=True)  5.75 us
    ppermute x4, starting transfers between devices, passed_along(): return lax.ppermute(value, axis, pairs)  5.47 us
  transfers between devices with their start and end apart: 8, of which 3 were waited for; matrix products, arithmetic and copies ran while one was open for 41% of the time, Pallas kernels for 0%

profile of v1, /device:TPU:0, one launch (start us, length us, event | category | flops | bytes accessed | tf_op | source)
XLA Modules:
  0.0 175.8 jit_solution(2172555163234582554)
XLA Ops:
  1.9 2.2 %fusion.35 = (f32[16,256]{1,0:T(8,128)S(1)}, f32[16,256,128]{2,1,0:T(8,128)S(1)}) fusion(f32[16,256,128]{2,1,0:T(8,128)} %param.8, f32[256,128]{1,0:T(8,128)S(1)} %mul.121), kind=kLoop, calls=%fused_computation.63 | loop fusion | flops 1044480 | bytes 4341760 | tf_op jit(solution)/shard_map/reduce_sum | solution.py:35
  4.2 9.7 %all-gather = f32[64,256]{1,0:T(8,128)S(1)} all-gather(f32[16,256]{1,0:T(8,128)S(1)} %get-tuple-element.35), channel_id=2, replica_groups=mesh['light'=4,'screen'=8] {'light'}, dimensions={0}, use_global_device_ids=true | all-gather | bytes 81920 | tf_op jit(solution)/shard_map/all_gather | solution.py:17
  14.6 3.8 %exponential_multiply_fusion = f32[16,256,128]{2,1,0:T(8,128)S(1)} fusion(f32[16,256,128]{2,1,0:T(8,128)} %param.9, f32[16,256,128]{2,1,0:T(8,128)S(1)} %get-tuple-element.36, f32[16,256]{1,0:T(8,128)S(1)} %get-tuple-element.26, f32[16,256]{1,0:T(8,128)S(1)} %sub.66, f32[16,256]{1,0:T(8,128)S(1)} %constant_dynamic-slice_fusion), kind=kOutput, calls=%fused_computation.43 | convolution fusion | flops 807944192 | bytes 6340608 | tf_op jit(solution)/shard_map/dot_general | solution.py:34
  19.8 2.5 %copy.36 = f32[16,256,128]{2,0,1:T(8,128)} copy(f32[16,256,128]{2,1,0:T(8,128)S(1)} %exponential_multiply_fusion) | data formatting | bytes 4194304 | tf_op jit(solution)/shard_map/mul | solution.py:120
  22.4 5.7 %all-to-all-start.2 = ((f32[16,256,128]{2,0,1:T(8,128)}), f32[16,256,128]{2,0,1:T(8,128)}, u32[]{:S(2)}, u32[]{:S(2)}) async-start(f32[16,256,128]{2,0,1:T(8,128)} %copy.36), calls=%async_computation.2 | async-start | bytes 4194304 | tf_op jit(solution)/shard_map/all_to_all | solution.py:121
  28.1 8.5 %reshape.96 = f32[1,16,16,16,8,16]{5,4,3,2,1,0:T(8,128)} reshape(f32[16,256,128]{2,1,0:T(8,128)S(1)} %copy-done.8) | data formatting | bytes 4194304 | tf_op jit(solution)/shard_map/reshape | solution.py:112
  36.6 1.9 %slice_multiply_fusion = f32[1,2,16,16,8,16]{5,4,3,2,1,0:T(8,128)S(1)} fusion(f32[1,16,16,16,8,16]{5,4,3,2,1,0:T(8,128)} %reshape.96, f32[16,8]{1,0:T(8,128)S(1)} %copy.28), kind=kLoop, calls=%fused_computation.41 | loop fusion | flops 65536 | bytes 524800 | tf_op jit(solution)/shard_map/mul | solution.py:112
  42.8 1.7 pad_maximum_fusion.1
  44.5 1.7 pad_slice_fusion.3
  46.2 2.7 %copy.33 = f32[18,258,1]{1,2,0:T(1,128)S(1)} copy(f32[18,258,1]{2,1,0:T(8,128)} %pad_slice_fusion.3) | data formatting | bytes 37152 | tf_op jit(solution)/shard_map/slice | solution.py:95
  50.2 1.7 pad_maximum_fusion
  53.4 1.6 pad_slice_fusion.5
  55.0 2.7 %copy.30 = f32[18,258,1]{1,2,0:T(1,128)S(1)} copy(f32[18,258,1]{2,1,0:T(8,128)} %pad_slice_fusion.5) | data formatting | bytes 37152 | tf_op jit(solution)/shard_map/slice | solution.py:95
  59.3 2.2 %pad_slice_fusion.2 = f32[18,256,127]{2,1,0:T(8,128)} fusion(f32[18,256,128]{2,1,0:T(8,128)S(1)} %pad_maximum_fusion.1), kind=kLoop, calls=%fused_computation.25 | loop fusion | bytes 4700160 | tf_op jit(solution)/shard_map/slice | solution.py:65
  61.5 2.1 %pad_slice_fusion.4 = f32[18,256,127]{2,1,0:T(8,128)} fusion(f32[18,256,128]{2,1,0:T(8,128)S(1)} %copy-done.3), kind=kLoop, calls=%fused_computation.27 | loop fusion | bytes 4700160 | tf_op jit(solution)/shard_map/slice | solution.py:65
  63.6 2.1 %fusion.3 = f32[18,256,127]{2,1,0:T(8,128)} fusion(f32[2,256,128]{2,1,0:T(8,128)S(1)} %collective-permute-done.2, f32[16,256,128]{2,1,0:T(8,128)S(1)} %copy-done.5), kind=kLoop, calls=%fused_computation.9 | loop fusion | flops 585216 | bytes 4700160 | tf_op jit(solution)/shard_map/concatenate | solution.py:94
  65.8 2.1 %fusion.4 = f32[18,256,127]{2,1,0:T(8,128)} fusion(f32[2,256,128]{2,1,0:T(8,128)S(1)} %collective-permute-done, f32[16,256,128]{2,1,0:T(8,128)S(1)} %copy-done.7), kind=kLoop, calls=%fused_computation.10 | loop fusion | flops 585216 | bytes 4700160 | tf_op jit(solution)/shard_map/concatenate | solution.py:93
  68.0 2.1 %copy.35 = f32[18,256,1]{2,1,0:T(8,128)} copy(f32[18,256,1]{1,2,0:T(1,128)S(1)} %get-tuple-element.48) | data formatting | bytes 36864 | tf_op jit(solution)/shard_map/slice | solution.py:63
  70.1 2.1 %copy.34 = f32[18,256,1]{2,1,0:T(8,128)} copy(f32[18,256,1]{1,2,0:T(1,128)S(1)} %get-tuple-element.49) | data formatting | bytes 36864 | tf_op jit(solution)/shard_map/slice | solution.py:62
  72.4 2.1 %copy.32 = f32[18,256,1]{2,1,0:T(8,128)} copy(f32[18,256,1]{1,2,0:T(1,128)S(1)} %get-tuple-element.50) | data formatting | bytes 36864 | tf_op jit(solution)/shard_map/slice | solution.py:63
  74.5 2.2 %copy.31 = f32[18,256,1]{2,1,0:T(8,128)} copy(f32[18,256,1]{1,2,0:T(1,128)S(1)} %get-tuple-element.51) | data formatting | bytes 36864 | tf_op jit(solution)/shard_map/slice | solution.py:62
  76.7 11.8 %fusion.14 = (f32[18,256,128]{2,1,0:T(8,128)}, f32[18,256,128]{2,1,0:T(8,128)S(1)}) fusion(f32[18,256,1]{2,1,0:T(8,128)} %copy.34, f32[18,256,127]{2,1,0:T(8,128)} %fusion.3, f32[18,256,1]{2,1,0:T(8,128)} %copy.35, f32[18,256,127]{2,1,0:T(8,128)} %pad_slice_fusion.2, f32[18,256,128]{2,1,0:T(8,128)S(1)} %pad_maximum_fusion.1, f32[256,128]{1,0:T(8,128)S(1)} %bitcast.79, ...), kind=kLoop, calls=%fused_computation.24 | loop fusion | flops 12976128 | bytes 19136512 | tf_op jit(solution)/shard_map/add | solution.py:71
  90.5 2.5 %fusion.24 = f32[2,8,256,128]{3,1,2,0:T(8,128)S(1)} fusion(f32[2,8,256,128]{3,2,1,0:T(8,128)S(1)} %bitcast.69, f32[32768]{0:T(1024)S(1)} %subtract_bitcast_fusion), kind=kOutput, calls=%fused_computation.46 | convolution fusion | flops 101712128 | bytes 4325376 | tf_op jit(solution)/shard_map/ij,bjr->bir/dot_general | solution.py:47
  93.0 1.7 copy.45
  94.7 31.0 %all-to-all-start = ((f32[1,256,128]{2,0,1:T(1,128)}), f32[1,256,128]{2,0,1:T(1,128)S(1)}, u32[]{:S(2)}, u32[]{:S(2)}) async-start(f32[1,256,128]{2,0,1:T(1,128)} %bitcast.7), calls=%async_computation | async-start | bytes 262144 | tf_op jit(solution)/shard_map/all_to_all | solution.py:103
  125.7 4.3 %fusion.16 = f32[256,128]{1,0:T(8,128)} fusion(f32[2,8,256,128]{3,2,1,0:T(8,128)} %copy.45, f32[18,256,128]{2,1,0:T(8,128)} %get-tuple-element.46, f32[16,256,128]{2,1,0:T(8,128)S(1)} %get-tuple-element.38, f32[256,128]{1,0:T(8,128)S(1)} %bitcast.78), kind=kLoop, calls=%fused_computation.31 | loop fusion | flops 4161536 | bytes 8650752 | tf_op jit(solution)/shard_map/reduce_sum | solution.py:79
  130.0 2.3 %copy.37 = f32[16,256,128]{2,1,0:T(8,128)S(1)} copy(f32[16,256,128]{2,0,1:T(8,128)} %all-to-all-done.2) | data formatting | bytes 4194304 | tf_op jit(solution)/shard_map/all_to_all | solution.py:121
  132.5 4.9 %all-to-all-start.1 = ((f32[1,256,128]{2,0,1:T(1,128)}), f32[1,256,128]{2,0,1:T(1,128)S(1)}, u32[]{:S(2)}, u32[]{:S(2)}) async-start(f32[1,256,128]{2,0,1:T(1,128)} %bitcast.14), calls=%async_computation.1 | async-start | bytes 262144 | tf_op jit(solution)/shard_map/all_to_all | solution.py:102
  139.3 4.9 %all-to-all-done.1 = f32[1,256,128]{2,0,1:T(1,128)S(1)} async-done(((f32[1,256,128]{2,0,1:T(1,128)}), f32[1,256,128]{2,0,1:T(1,128)S(1)}, u32[]{:S(2)}, u32[]{:S(2)}) %all-to-all-start.1) | async-done | bytes 131104 | tf_op jit(solution)/shard_map/all_to_all | solution.py:102
  144.2 4.6 %all-to-all-start.3 = ((f32[4,32,32,128]{3,2,1,0:T(8,128)}), f32[4,32,32,128]{3,2,1,0:T(8,128)S(1)}, u32[]{:S(2)}, u32[]{:S(2)}) async-start(f32[4,32,32,128]{3,2,1,0:T(8,128)} %pad_maximum_fusion.4), calls=%async_computation.3 | async-start | bytes 4194304 | tf_op jit(solution)/shard_map/all_to_all | solution.py:123
  150.1 24.1 %all-to-all-done.3 = f32[4,32,32,128]{3,2,1,0:T(8,128)S(1)} async-done(((f32[4,32,32,128]{3,2,1,0:T(8,128)}), f32[4,32,32,128]{3,2,1,0:T(8,128)S(1)}, u32[]{:S(2)}, u32[]{:S(2)}) %all-to-all-start.3) | async-done | bytes 2097184 | tf_op jit(solution)/shard_map/all_to_all | solution.py:123
  174.2 1.6 copy_bitcast_fusion
  (60 shorter events, 17.4 us)
Async XLA Ops:
  0.6 40.4 %copy-start = (s32[256,512]{1,0:T(8,128)S(1)}, s32[256,512]{1,0:T(8,128)}, u32[]{:S(2)}) copy-start(s32[256,512]{1,0:T(8,128)} %param.12) | copy-start | bytes 1572868
  4.1 14.3 %copy-start.6 = (f32[16,256,128]{2,1,0:T(8,128)}, f32[16,256,128]{2,1,0:T(8,128)S(1)}, u32[]{:S(2)}) copy-start(f32[16,256,128]{2,1,0:T(8,128)S(1)} %get-tuple-element.36) | copy-start | bytes 6291460
  18.5 1.3 copy-start.4
  18.5 24.3 %collective-permute-start.2 = (f32[2,256,128]{2,1,0:T(8,128)S(1)}, f32[2,256,128]{2,1,0:T(8,128)S(1)}, u32[]{:S(2)}, u32[]{:S(2)}) collective-permute-start(f32[2,256,128]{2,1,0:T(8,128)S(1)} %slice.109), channel_id=1, source_target_pairs={{1,0},{2,1},{3,2},{4,3},{5,4},{6,5},{7,6},{9,8},{10,9},{11,10},{12... | collective-permute-start | bytes 786440 | tf_op jit(solution)/shard_map/ppermute | solution.py:12
  22.4 5.8 %copy-start.8 = (f32[16,256,128]{2,1,0:T(8,128)S(1)}, f32[16,256,128]{2,1,0:T(8,128)}, u32[]{:S(2)}) copy-start(f32[16,256,128]{2,1,0:T(8,128)} %param.8) | copy-start | bytes 6291460
  22.4 72.3 %all-to-all-start.2 = ((f32[16,256,128]{2,0,1:T(8,128)}), f32[16,256,128]{2,0,1:T(8,128)}, u32[]{:S(2)}, u32[]{:S(2)}) async-start(f32[16,256,128]{2,0,1:T(8,128)} %copy.36), calls=%async_computation.2 | async-start | bytes 4194304 | tf_op jit(solution)/shard_map/all_to_all | solution.py:121
  38.5 2.6 %copy-start.11 = (f32[3,16]{1,0:T(4,128)S(1)}, f32[3,16]{1,0:T(4,128)}, u32[]{:S(2)}) copy-start(f32[3,16]{1,0:T(4,128)} %param.13) | copy-start | bytes 580
  39.7 10.4 %collective-permute-start = (f32[2,256,128]{2,1,0:T(8,128)}, f32[2,256,128]{2,1,0:T(8,128)S(1)}, u32[]{:S(2)}, u32[]{:S(2)}) collective-permute-start(f32[2,256,128]{2,1,0:T(8,128)} %slice.78), channel_id=1, source_target_pairs={{1,0},{2,1},{3,2},{4,3},{5,4},{6,5},{7,6},{9,8},{10,9},{11,10},{12... | collective-permute-start | bytes 786440 | tf_op jit(solution)/shard_map/ppermute | solution.py:12
  48.9 19.0 %collective-permute-start.3 = (f32[18,258,1]{1,2,0:T(1,128)S(1)}, f32[18,258,1]{1,2,0:T(1,128)S(1)}, u32[]{:S(2)}, u32[]{:S(2)}) collective-permute-start(f32[18,258,1]{1,2,0:T(1,128)S(1)} %copy.33), channel_id=1, source_target_pairs={{8,0},{16,8},{24,16},{9,1},{17,9},{25,17},{10,2},{18,10},{26,18},{... | collective-permute-start | bytes 55736 | tf_op jit(solution)/shard_map/ppermute | solution.py:12
  51.9 1.5 copy-start.2
  57.7 3.8 %copy-start.3 = (f32[18,256,128]{2,1,0:T(8,128)S(1)}, f32[18,256,128]{2,1,0:T(8,128)}, u32[]{:S(2)}) copy-start(f32[18,256,128]{2,1,0:T(8,128)} %copy-done.2) | copy-start | bytes 7077892
  57.7 14.5 %collective-permute-start.1 = (f32[18,258,1]{1,2,0:T(1,128)S(1)}, f32[18,258,1]{1,2,0:T(1,128)S(1)}, u32[]{:S(2)}, u32[]{:S(2)}) collective-permute-start(f32[18,258,1]{1,2,0:T(1,128)S(1)} %copy.30), channel_id=1, source_target_pairs={{8,0},{16,8},{24,16},{9,1},{17,9},{25,17},{10,2},{18,10},{26,18},{... | collective-permute-start | bytes 55736 | tf_op jit(solution)/shard_map/ppermute | solution.py:12
  61.5 2.1 %copy-start.5 = (f32[16,256,128]{2,1,0:T(8,128)S(1)}, f32[16,256,128]{2,1,0:T(8,128)}, u32[]{:S(2)}) copy-start(f32[16,256,128]{2,1,0:T(8,128)} %copy-done.4) | copy-start | bytes 6291460
  63.6 2.1 %copy-start.7 = (f32[16,256,128]{2,1,0:T(8,128)S(1)}, f32[16,256,128]{2,1,0:T(8,128)}, u32[]{:S(2)}) copy-start(f32[16,256,128]{2,1,0:T(8,128)} %copy-done.6) | copy-start | bytes 6291460
  72.3 4.4 %copy-start.9 = (f32[1,256,128]{2,0,1:T(1,128)S(1)}, f32[1,256,128]{2,0,1:T(1,128)}, u32[]{:S(2)}) copy-start(f32[1,256,128]{2,0,1:T(1,128)} %get-tuple-element.44) | copy-start | bytes 393220
  72.3 4.4 %copy-start.10 = (f32[1,256,128]{2,0,1:T(1,128)S(1)}, f32[1,256,128]{2,0,1:T(1,128)}, u32[]{:S(2)}) copy-start(f32[1,256,128]{2,0,1:T(1,128)} %get-tuple-element.45) | copy-start | bytes 393220
  94.7 37.8 %all-to-all-start = ((f32[1,256,128]{2,0,1:T(1,128)}), f32[1,256,128]{2,0,1:T(1,128)S(1)}, u32[]{:S(2)}, u32[]{:S(2)}) async-start(f32[1,256,128]{2,0,1:T(1,128)} %bitcast.7), calls=%async_computation | async-start | bytes 262144 | tf_op jit(solution)/shard_map/all_to_all | solution.py:103
  132.5 11.7 %all-to-all-start.1 = ((f32[1,256,128]{2,0,1:T(1,128)}), f32[1,256,128]{2,0,1:T(1,128)S(1)}, u32[]{:S(2)}, u32[]{:S(2)}) async-start(f32[1,256,128]{2,0,1:T(1,128)} %bitcast.14), calls=%async_computation.1 | async-start | bytes 262144 | tf_op jit(solution)/shard_map/all_to_all | solution.py:102
  144.2 30.0 %all-to-all-start.3 = ((f32[4,32,32,128]{3,2,1,0:T(8,128)}), f32[4,32,32,128]{3,2,1,0:T(8,128)S(1)}, u32[]{:S(2)}, u32[]{:S(2)}) async-start(f32[4,32,32,128]{3,2,1,0:T(8,128)} %pad_maximum_fusion.4), calls=%async_computation.3 | async-start | bytes 4194304 | tf_op jit(solution)/shard_map/all_to_all | solution.py:123
  148.8 27.0 %copy-start.1 = (s32[256,512]{1,0:T(8,128)S(1)}, s32[256,512]{1,0:T(8,128)}, u32[]{:S(2)}) copy-start(s32[256,512]{1,0:T(8,128)} %param.12) | copy-start | bytes 1572868
